TPU v7x, 32 devices: a whole 2x2x4 slice. The times are simulated.
32 devices in a mesh: row: 8 (over z, x), col: 4 (over y, core).
Axes of the slice: x: 2, y: 2, z: 4, core: 2. Of those that a mesh axis runs over, the one named last changes fastest.
Arguments:
- acquired_tiles: bfloat16 [4, 32768, 1024], P(None, ('row', 'col')), may hold values from -24 to 24
- row_live: int32 [4, 32768], P(None, ('row', 'col')), may hold values from 0 to 1, as said below
- col_live: int32 [4, 32768], P(None, ('row', 'col')), may hold values 0 or 1
- row_order: int32 [8], replicated, may hold values from 0 to 7, as said below
- source_init: float32 [32768, 256], P(('row', 'col')), may hold values from -3 to 3
- receiver_init: float32 [32768, 256], P(('row', 'col')), may hold values from -3 to 3
Outputs:
- sources: float32 [32768, 256], P(('row', 'col'))
- receivers: float32 [32768, 256], P(('row', 'col'))
Inputs may be any that keep to these rules, and one draw needn't show every extreme that they name: `row_live`: 1 where the source of that row is recorded in that stratum's tile; sources go missing singly and in whole aligned lines of 128 rows, and the share of missing lines differs from block to block. `row_order`: each number once.
All inputs are finite; a program needn't handle non-finite values. No bound on the sum of `col_live` on one device may be relied on, other than what follows from the above.
Results may differ from a plain program's by a relative error of at most 0.00096.
Values sent between devices are 32-bit elements; how exact they have to be, the bound alone decides.
A program may use at most 128 MiB of HBM per device.

v0:
```python
import jax
import jax.numpy as jnp
from jax import lax
from jax.sharding import PartitionSpec as P

STEPS = 2


def from_behind(block, axis, distance):
    devices = range(lax.axis_size(axis))
    route = [((i - distance) % len(devices), i) for i in devices]
    return lax.ppermute(block, axis, route)


def fit_dense(src_block, rec_block, acquired, live_rows, live_cols):
    weights = live_rows.astype(jnp.float32)[:, None] * live_cols.astype(jnp.float32)[None, :]
    observed = acquired.astype(jnp.float32)
    step_size = 1.0 / (acquired.shape[1] + 2 * src_block.shape[1])
    for iteration in range(STEPS):
        src_half = src_block.astype(jnp.bfloat16)
        rec_half = rec_block.astype(jnp.bfloat16)
        predicted = lax.dot_general(
            src_half, rec_half, (((1,), (1,)), ((), ())), preferred_element_type=jnp.float32
        )
        misfit = (weights * (observed - predicted)).astype(jnp.bfloat16)
        grad_src = jnp.dot(misfit, rec_half, preferred_element_type=jnp.float32)
        grad_rec = lax.dot_general(
            misfit, src_half, (((0,), (0,)), ((), ())), preferred_element_type=jnp.float32
        )
        src_block = src_block + step_size * grad_src
        rec_block = rec_block + step_size * grad_rec
    return (src_block, rec_block)


def reassign(rec_block, row_order):
    block_rows, rank_width = rec_block.shape
    pieces = lax.all_to_all(
        rec_block.reshape(1, block_rows, rank_width), "row", split_axis=1, concat_axis=0, tiled=True
    )
    pieces = jnp.take(pieces, row_order, axis=0)
    returned = lax.all_to_all(pieces, "row", split_axis=0, concat_axis=1, tiled=True)
    return returned.reshape(block_rows, rank_width)


def local(acquired_tiles, row_live, col_live, row_order, source_init, receiver_init):
    src_block = source_init
    rec_block = receiver_init
    strata = acquired_tiles.shape[0]
    for stratum in range(strata):
        src_block, rec_block = fit_dense(
            src_block, rec_block, acquired_tiles[stratum], row_live[stratum], col_live[stratum]
        )
        if stratum + 1 < strata:
            rec_block = from_behind(rec_block, ("row", "col"), 1)
            if stratum == 1:
                rec_block = reassign(rec_block, row_order)
    return (src_block, rec_block)


def solution(mesh):
    placed = (
        P(None, ("row", "col"), None),
        P(None, ("row", "col")),
        P(None, ("row", "col")),
        P(),
        P(("row", "col"), None),
        P(("row", "col"), None),
    )
    return jax.shard_map(
        local,
        mesh=mesh,
        in_specs=placed,
        out_specs=(P(("row", "col"), None), P(("row", "col"), None)),
        check_vma=False,
    )
```

profile of v0, /device:TPU:0, one launch (start us, length us, event | category | flops | bytes accessed | tf_op | source)
XLA Modules:
  0.0 149.0 jit_solution(8501711927796989508)
XLA Ops:
  2.4 3.2 %fusion = bf16[1024,1024]{1,0:T(8,128)(2,1)S(1)} fusion(f32[1024]{0:T(1024)S(1)} %bitcast.62, f32[1024]{0:T(1024)S(1)} %bitcast.60, bf16[4,1024,1024]{2,1,0:T(8,128)(2,1)} %param.6, f32[1024,256]{1,0:T(8,128)} %param.11, f32[1024,256]{1,0:T(8,128)} %param.10), kind=kOutput, calls=%fused_computation.17 | convolution fusion | flops 542638080 | bytes 6299648 | tf_op jit(solution)/shard_map/dot_general | solution.py:22
  7.9 1.5 slice-done.1
  9.4 0.9 fusion.1
  12.3 17.7 %collective-permute-done = f32[1024,256]{1,0:T(8,128)S(1)} collective-permute-done((f32[1024,256]{1,0:T(8,128)S(1)}, f32[1024,256]{1,0:T(8,128)S(1)}, u32[]{:S(2)}, u32[]{:S(2)}) %collective-permute-start) | collective-permute-done | bytes 1048608 | tf_op jit(solution)/shard_map/ppermute | solution.py:12
  30.0 0.9 fusion.2
  34.2 17.8 %collective-permute-done.1 = f32[1024,256]{1,0:T(8,128)S(1)} collective-permute-done((f32[1024,256]{1,0:T(8,128)S(1)}, f32[1024,256]{1,0:T(8,128)S(1)}, u32[]{:S(2)}, u32[]{:S(2)}) %collective-permute-start.1) | collective-permute-done | bytes 1048608 | tf_op jit(solution)/shard_map/ppermute | solution.py:12
  52.0 2.0 %copy.8 = f32[1,1024,256]{2,0,1:T(1,128)} copy(f32[1,1024,256]{2,1,0:T(8,128)S(1)} %bitcast.47) | data formatting | bytes 2097152 | tf_op jit(solution)/shard_map/reshape | solution.py:38
  54.0 4.2 %all-to-all-start = ((f32[1,1024,256]{2,0,1:T(1,128)}), f32[1,1024,256]{2,0,1:T(1,128)}, u32[]{:S(2)}, u32[]{:S(2)}) async-start(f32[1,1024,256]{2,0,1:T(1,128)} %copy.8), calls=%async_computation | async-start | bytes 2097152 | tf_op jit(solution)/shard_map/all_to_all | solution.py:37
  58.3 20.2 %all-to-all-done = f32[1,1024,256]{2,0,1:T(1,128)} async-done(((f32[1,1024,256]{2,0,1:T(1,128)}), f32[1,1024,256]{2,0,1:T(1,128)}, u32[]{:S(2)}, u32[]{:S(2)}) %all-to-all-start) | async-done | bytes 1048608 | tf_op jit(solution)/shard_map/all_to_all | solution.py:37
  78.5 2.3 %copy.9 = f32[1,1024,256]{2,1,0:T(8,128)} copy(f32[1,1024,256]{2,0,1:T(1,128)} %all-to-all-done) | data formatting | bytes 2097152
  80.8 2.8 %gather_fusion = f32[8,128,256]{2,1,0:T(8,128)} fusion(f32[8,128,256]{2,1,0:T(8,128)} %bitcast.46, s32[1024]{0:T(1024)S(1)} %pad_clamp_fusion), kind=kCustom, calls=%fused_computation | custom fusion | bytes 2097184 | tf_op jit(solution)/shard_map/jit(_take)/gather | solution.py:40
  83.6 2.4 %broadcast_select_fusion = f32[8,128,256]{2,1,0:T(8,128)} fusion(f32[8,128,256]{2,1,0:T(8,128)} %gather_fusion, pred[8]{0:T(512)(128)(4,1)S(1)} %compare_and_fusion), kind=kLoop, calls=%fused_computation.58 | loop fusion | flops 262144 | bytes 2097160 | tf_op jit(solution)/shard_map/jit(_take)/select_n | solution.py:40
  86.0 4.4 %all-to-all-start.1 = ((f32[8,128,256]{2,1,0:T(8,128)}), f32[8,128,256]{2,1,0:T(8,128)}, u32[]{:S(2)}, u32[]{:S(2)}) async-start(f32[8,128,256]{2,1,0:T(8,128)} %broadcast_select_fusion), calls=%async_computation.1 | async-start | bytes 2097152 | tf_op jit(solution)/shard_map/all_to_all | solution.py:41
  90.4 2.9 %fusion.17 = f32[1024,256]{1,0:T(8,128)} fusion(f32[1024,256]{1,0:T(8,128)S(1)} %fusion.19, bf16[1024,1024]{1,0:T(8,128)(2,1)S(1)} %fusion.3, f32[1024,256]{1,0:T(8,128)} %copy-done.1), kind=kOutput, calls=%fused_computation.44 | convolution fusion | flops 537657344 | bytes 5242880 | tf_op jit(solution)/shard_map/dot_general | solution.py:26
  93.3 19.2 %all-to-all-done.1 = f32[8,128,256]{2,1,0:T(8,128)} async-done(((f32[8,128,256]{2,1,0:T(8,128)}), f32[8,128,256]{2,1,0:T(8,128)}, u32[]{:S(2)}, u32[]{:S(2)}) %all-to-all-start.1) | async-done | bytes 1048608 | tf_op jit(solution)/shard_map/all_to_all | solution.py:41
  112.5 1.3 bitcast_convert_fusion
  113.8 2.9 %fusion.4 = bf16[1024,1024]{1,0:T(8,128)(2,1)S(1)} fusion(bf16[1024,256]{1,0:T(8,128)(2,1)S(1)} %bitcast_convert_fusion, f32[1024]{0:T(1024)S(1)} %bitcast.54, f32[1024]{0:T(1024)S(1)} %bitcast.52, bf16[4,1024,1024]{2,1,0:T(8,128)(2,1)} %param.6, f32[1024,256]{1,0:T(8,128)} %fusion.17), kind=kOutput, calls=%fused_computation.21 | convolution fusion | flops 542375936 | bytes 5775360 | tf_op jit(solution)/shard_map/dot_general | solution.py:22
  117.5 2.3 %fusion.14 = f32[1024,256]{1,0:T(8,128)S(1)} fusion(f32[1024,256]{1,0:T(8,128)} %bitcast.12, bf16[1024,1024]{1,0:T(8,128)(2,1)S(1)} %fusion.4, f32[1024,256]{1,0:T(8,128)S(1)} %copy-done), kind=kOutput, calls=%fused_computation.38 | convolution fusion | flops 537657344 | bytes 5242880 | tf_op jit(solution)/shard_map/dot_general | solution.py:27
  119.8 0.9 fusion.5
  122.3 20.0 %collective-permute-done.2 = f32[1024,256]{1,0:T(8,128)S(1)} collective-permute-done((f32[1024,256]{1,0:T(8,128)S(1)}, f32[1024,256]{1,0:T(8,128)S(1)}, u32[]{:S(2)}, u32[]{:S(2)}) %collective-permute-start.2) | collective-permute-done | bytes 1048608 | tf_op jit(solution)/shard_map/ppermute | solution.py:12
  142.2 0.9 fusion.6
  144.6 0.9 fusion.7
  145.6 1.7 %fusion.8 = f32[1024,256]{1,0:T(8,128)} fusion(f32[1024,256]{1,0:T(8,128)S(1)} %fusion.10, bf16[1024,1024]{1,0:T(8,128)(2,1)S(1)} %fusion.7, f32[1024,256]{1,0:T(8,128)S(1)} %fusion.11), kind=kOutput, calls=%fused_computation.26 | convolution fusion | flops 537657344 | bytes 5242880 | tf_op jit(solution)/shard_map/dot_general | solution.py:27
  147.3 1.7 %fusion.9 = f32[1024,256]{1,0:T(8,128)} fusion(f32[1024,256]{1,0:T(8,128)S(1)} %fusion.11, bf16[1024,1024]{1,0:T(8,128)(2,1)S(1)} %fusion.7, f32[1024,256]{1,0:T(8,128)S(1)} %fusion.10), kind=kOutput, calls=%fused_computation.28 | convolution fusion | flops 537657344 | bytes 5242880 | tf_op jit(solution)/shard_map/dot_general | solution.py:26
  (40 shorter events, 12.9 us)
Async XLA Ops:
  2.4 3.3 %copy-start.2 = (f32[1024,256]{1,0:T(8,128)S(1)}, f32[1024,256]{1,0:T(8,128)}, u32[]{:S(2)}) copy-start(f32[1024,256]{1,0:T(8,128)} %param.10) | copy-start | bytes 3145732
  2.4 3.3 %copy-start.3 = (f32[1024,256]{1,0:T(8,128)S(1)}, f32[1024,256]{1,0:T(8,128)}, u32[]{:S(2)}) copy-start(f32[1024,256]{1,0:T(8,128)} %param.11) | copy-start | bytes 3145732
  5.7 2.2 %slice-start = ((s8[8388608]{0:T(1024)(128)(4,1)}), s8[4194304]{0:T(1024)(128)(4,1)S(1)}, s32[]{:S(2)}) async-start(s8[8388608]{0:T(1024)(128)(4,1)} %bitcast.64), calls=%async_computation.2 | async-start | bytes 8388608
  6.5 2.9 %slice-start.1 = ((s8[8388608]{0:T(1024)(128)(4,1)}), s8[4194304]{0:T(1024)(128)(4,1)S(1)}, s32[]{:S(2)}) async-start(s8[8388608]{0:T(1024)(128)(4,1)} %bitcast.64), calls=%async_computation.3 | async-start | bytes 8388608
  11.0 18.9 %collective-permute-start = (f32[1024,256]{1,0:T(8,128)S(1)}, f32[1024,256]{1,0:T(8,128)S(1)}, u32[]{:S(2)}, u32[]{:S(2)}) collective-permute-start(f32[1024,256]{1,0:T(8,128)S(1)} %fusion.20), channel_id=1, source_target_pairs={{31,0},{0,1},{1,2},{2,3},{3,4},{4,5},{5,6},{6,7},{7,8},{8,9},{9,10... | collective-permute-start | bytes 3145736 | tf_op jit(solution)/shard_map/ppermute | solution.py:12
  31.7 1.7 %copy-start.1 = (f32[1024,256]{1,0:T(8,128)}, f32[1024,256]{1,0:T(8,128)S(1)}, u32[]{:S(2)}) copy-start(f32[1024,256]{1,0:T(8,128)S(1)} %fusion.18) | copy-start | bytes 3145732
  34.1 17.9 %collective-permute-start.1 = (f32[1024,256]{1,0:T(8,128)S(1)}, f32[1024,256]{1,0:T(8,128)S(1)}, u32[]{:S(2)}, u32[]{:S(2)}) collective-permute-start(f32[1024,256]{1,0:T(8,128)S(1)} %fusion.16), channel_id=1, source_target_pairs={{31,0},{0,1},{1,2},{2,3},{3,4},{4,5},{5,6},{6,7},{7,8},{8,9},{9,10... | collective-permute-start | bytes 3145736 | tf_op jit(solution)/shard_map/ppermute | solution.py:12
  52.0 6.3 %copy-start.4 = (s32[8]{0:T(128)S(1)}, s32[8]{0:T(128)}, u32[]{:S(2)}) copy-start(s32[8]{0:T(128)} %param.9) | copy-start | bytes 100
  54.0 24.5 %all-to-all-start = ((f32[1,1024,256]{2,0,1:T(1,128)}), f32[1,1024,256]{2,0,1:T(1,128)}, u32[]{:S(2)}, u32[]{:S(2)}) async-start(f32[1,1024,256]{2,0,1:T(1,128)} %copy.8), calls=%async_computation | async-start | bytes 2097152 | tf_op jit(solution)/shard_map/all_to_all | solution.py:37
  86.0 26.5 %all-to-all-start.1 = ((f32[8,128,256]{2,1,0:T(8,128)}), f32[8,128,256]{2,1,0:T(8,128)}, u32[]{:S(2)}, u32[]{:S(2)}) async-start(f32[8,128,256]{2,1,0:T(8,128)} %broadcast_select_fusion), calls=%async_computation.1 | async-start | bytes 2097152 | tf_op jit(solution)/shard_map/all_to_all | solution.py:41
  113.7 3.0 %copy-start = (f32[1024,256]{1,0:T(8,128)S(1)}, f32[1024,256]{1,0:T(8,128)}, u32[]{:S(2)}) copy-start(f32[1024,256]{1,0:T(8,128)} %fusion.17) | copy-start | bytes 3145732
  113.8 6.0 %slice-start.2 = ((s8[8388608]{0:T(1024)(128)(4,1)}), s8[4194304]{0:T(1024)(128)(4,1)S(1)}, s32[]{:S(2)}) async-start(s8[8388608]{0:T(1024)(128)(4,1)} %bitcast.66), calls=%async_computation.4 | async-start | bytes 8388608
  116.7 3.0 %slice-start.3 = ((s8[8388608]{0:T(1024)(128)(4,1)}), s8[4194304]{0:T(1024)(128)(4,1)S(1)}, s32[]{:S(2)}) async-start(s8[8388608]{0:T(1024)(128)(4,1)} %bitcast.66), calls=%async_computation.5 | async-start | bytes 8388608
  121.5 20.8 %collective-permute-start.2 = (f32[1024,256]{1,0:T(8,128)S(1)}, f32[1024,256]{1,0:T(8,128)S(1)}, u32[]{:S(2)}, u32[]{:S(2)}) collective-permute-start(f32[1024,256]{1,0:T(8,128)S(1)} %fusion.12), channel_id=1, source_target_pairs={{31,0},{0,1},{1,2},{2,3},{3,4},{4,5},{5,6},{6,7},{7,8},{8,9},{9,10... | collective-permute-start | bytes 3145736 | tf_op jit(solution)/shard_map/ppermute | solution.py:12
where the time goes:
time: 150 us; the launch traced here: 149 us
  waiting for transfers between devices  94.8 us (63%)
  matrix products  29.1 us (19%)
  local copies, waits for them, and re-layouts  9.34 us (6%)
  starting transfers between devices  9.32 us (6%)
  other arithmetic  5.44 us (4%)
    ppermute x3, waiting for transfers between devices, from_behind(): return lax.ppermute(block, axis, route)  55.4 us
    all_to_all x1, waiting for transfers between devices, reassign(): lax.all_to_all(rec_block.reshape(1, block_rows, rank_width), 'row', split...  20.2 us
    all_to_all x1, waiting for transfers between devices, reassign(): lax.all_to_all(pieces, 'row', split_axis=0, concat_axis=1, tiled=True)  19.2 us
    dot_general x8, matrix products, fit_dense(): lax.dot_general(src_half, rec_half, (((1,), (1,)), ((), ())), preferred_e...  11.8 us
    dot_general x8, matrix products, fit_dense(): grad_src = jnp.dot(misfit, rec_half, preferred_element_type=jnp.float32)  8.88 us
    dot_general x8, matrix products, fit_dense(): lax.dot_general(misfit, src_half, (((0,), (0,)), ((), ())), preferred_ele...  8.48 us
    unnamed x19, local copies, waits for them, and re-layouts  4.48 us
    all_to_all x1, starting transfers between devices, reassign(): lax.all_to_all(pieces, 'row', split_axis=0, concat_axis=1, tiled=True)  4.42 us
  transfers between devices with their start and end apart: 5, of which 5 were waited for; matrix products, arithmetic and copies ran while one was open for 3% of the time, Pallas kernels for 0%

commit v1 on v0

v1 whole, which is shorter than its diff:
```python
import functools

import jax
import jax.numpy as jnp
from jax import lax
from jax.experimental import pallas as pl
from jax.experimental.pallas import tpu as pltpu
from jax.sharding import PartitionSpec as P

STEPS = 2
MESH = pl.DeviceIdType.MESH
F32 = jnp.float32
BF16 = jnp.bfloat16


def kernel(nr, nc, tiles, row_live, col_live, order, src_in, rec_in, src_out, rec_out,
           tile, rb, mid, out2, grad, half, half_t, row_mask,
           in_sem, ring_send, ring_recv, a_send, a_recv, b_send, b_recv):
    strata, block, width = tile.shape
    rank = src_out.shape[1]
    chunk = rb.shape[2]
    chunks = width // chunk
    piece = mid.shape[1]
    per_chunk = nr // chunks
    step_size = 1.0 / (width + 2 * rank)
    r = lax.axis_index("row")
    c = lax.axis_index("col")
    cn = lax.rem(c + 1, nc)
    rn = lax.rem(r + (c + 1) // nc, nr)
    cp = lax.rem(c + nc - 1, nc)

    loads = [
        pltpu.make_async_copy(tiles.at[s], tile.at[s], in_sem.at[s]) for s in range(strata)
    ]
    for load in loads:
        load.start()

    barrier = pltpu.get_barrier_semaphore()
    for k in range(nr):
        pl.semaphore_signal(barrier, inc=1, device_id={"row": k, "col": cp}, device_id_type=MESH)
    for k in range(1, nr):
        pl.semaphore_signal(
            barrier, inc=1, device_id={"row": lax.rem(r + k, nr), "col": c}, device_id_type=MESH
        )

    src_out[...] = src_in[...]
    for q in range(chunks):
        rb[0, q * rank:(q + 1) * rank, :] = rec_in[q * chunk:(q + 1) * chunk, :].T

    def ring_copy(s, q):
        lane = 0 if s == 0 else 1
        rows = pl.ds(q * rank, rank)
        return pltpu.make_async_remote_copy(
            src_ref=rb.at[s, rows], dst_ref=rb.at[s + 1, rows],
            send_sem=ring_send.at[lane, q], recv_sem=ring_recv.at[lane, q],
            device_id={"row": rn, "col": cn}, device_id_type=MESH,
        )

    def a_copy(s, p, slot):
        return pltpu.make_async_remote_copy(
            src_ref=rb.at[s, pl.ds(p * piece, piece)], dst_ref=mid.at[slot],
            send_sem=a_send.at[p], recv_sem=a_recv.at[slot],
            device_id={"row": p, "col": cn}, device_id_type=MESH,
        )

    def b_copy(s, to, p):
        return pltpu.make_async_remote_copy(
            src_ref=out2.at[to], dst_ref=rb.at[s + 1, pl.ds(p * piece, piece)],
            send_sem=b_send.at[to], recv_sem=b_recv.at[p],
            device_id={"row": to, "col": c}, device_id_type=MESH,
        )

    for s in range(strata):
        lanes = row_live[s:s + 1, :].astype(F32)
        for t in range(block // 128):
            row_mask[t * 128:(t + 1) * 128, :] = jnp.broadcast_to(
                lanes[:, t * 128:(t + 1) * 128], (128, 128)
            ).T * step_size
        loads[s].wait()
        for it in range(STEPS):
            half[...] = src_out[...].astype(BF16)
            half_t[...] = (src_out[...].T * lanes).astype(BF16)

            def one(q, carry, s=s, it=it):
                rows = pl.ds(pl.multiple_of(q * rank, rank), rank)
                cols = pl.ds(pl.multiple_of(q * chunk, chunk), chunk)
                if it == 0 and s > 0:
                    if s == 2:
                        for j in range(per_chunk):
                            p = q * per_chunk + j

                            @pl.when(p != r)
                            def _():
                                b_copy(1, r, p).wait_recv()
                    else:
                        ring_copy(s - 1, q).wait_recv()
                rec = rb[s, rows, :]
                rec_half = rec.astype(BF16)
                live = col_live[s:s + 1, cols].astype(F32)
                predicted = jnp.dot(half[...], rec_half, preferred_element_type=F32)
                misfit = (tile[s, :, cols].astype(F32) - predicted).astype(BF16)
                grad_rec = jnp.dot(half_t[...], misfit, preferred_element_type=F32)
                rb[s, rows, :] = rec + (step_size * live) * grad_rec
                grad_src = lax.dot_general(
                    misfit, (rec_half * live.astype(BF16)), (((1,), (1,)), ((), ())),
                    preferred_element_type=F32,
                )

                @pl.when(q == 0)
                def _():
                    grad[...] = grad_src

                @pl.when(q > 0)
                def _():
                    grad[...] += grad_src

                if it == STEPS - 1 and s in (0, 2):
                    ring_copy(s, q).start()
                return carry

            if s == 0 and it == 0:
                pass
            if it == STEPS - 1 and s == 0:
                pl.semaphore_wait(barrier, 2 * nr - 1)
            lax.fori_loop(0, chunks, one, 0)
            if it == STEPS - 1 and s == 1:
                def send_a(k, carry):
                    p = lax.rem(r + k, nr)
                    a_copy(1, p, rn).start()
                    return carry
                lax.fori_loop(0, nr, send_a, 0)
            for h in range(rank // 128):
                part = slice(h * 128, (h + 1) * 128)
                src_out[:, part] = src_out[:, part] + row_mask[...] * grad[:, part]
        if s == 1:
            def wait_a(k, carry):
                a_copy(1, 0, k).wait_recv()
                return carry
            lax.fori_loop(0, nr, wait_a, 0)
            rb[2, pl.ds(pl.multiple_of(r * piece, piece), piece), :] = mid[order[r]]

            def pick(k, carry):
                to = lax.rem(r + k, nr)
                out2[to] = mid[order[to]]
                return carry
            lax.fori_loop(1, nr, pick, 0)

            def send_b(k, carry):
                b_copy(1, lax.rem(r + k, nr), r).start()
                return carry
            lax.fori_loop(1, nr, send_b, 0)

    for q in range(chunks):
        rec_out[q * chunk:(q + 1) * chunk, :] = rb[strata - 1, q * rank:(q + 1) * rank, :].T
    for s in (0, 2):
        for q in range(chunks):
            ring_copy(s, q).wait_send()

    def done_a(k, carry):
        a_copy(1, k, 0).wait_send()
        return carry
    lax.fori_loop(0, nr, done_a, 0)

    def done_b(k, carry):
        b_copy(1, lax.rem(r + k, nr), r).wait_send()
        return carry
    lax.fori_loop(1, nr, done_b, 0)


def local(nr, nc, tiles, row_live, col_live, row_order, source_init, receiver_init):
    strata, block, width = tiles.shape
    rank = source_init.shape[1]
    chunk = width // 4
    chunks = width // chunk
    piece = chunks * rank // nr
    vmem = pl.BlockSpec(memory_space=pltpu.VMEM)
    return pl.pallas_call(
        functools.partial(kernel, nr, nc),
        out_shape=(
            jax.ShapeDtypeStruct(source_init.shape, F32),
            jax.ShapeDtypeStruct(receiver_init.shape, F32),
        ),
        in_specs=[
            pl.BlockSpec(memory_space=pl.ANY), vmem, vmem,
            pl.BlockSpec(memory_space=pltpu.SMEM), vmem, vmem,
        ],
        out_specs=(vmem, vmem),
        scratch_shapes=[
            pltpu.VMEM((strata, block, width), BF16),
            pltpu.VMEM((strata, chunks * rank, chunk), F32),
            pltpu.VMEM((nr, piece, chunk), F32),
            pltpu.VMEM((nr, piece, chunk), F32),
            pltpu.VMEM((block, rank), F32),
            pltpu.VMEM((block, rank), BF16),
            pltpu.VMEM((rank, block), BF16),
            pltpu.VMEM((block, 128), F32),
            pltpu.SemaphoreType.DMA((strata,)),
            pltpu.SemaphoreType.DMA((2, chunks)),
            pltpu.SemaphoreType.DMA((2, chunks)),
            pltpu.SemaphoreType.DMA((nr,)),
            pltpu.SemaphoreType.DMA((nr,)),
            pltpu.SemaphoreType.DMA((nr,)),
            pltpu.SemaphoreType.DMA((nr,)),
        ],
        compiler_params=pltpu.CompilerParams(
            collective_id=0, has_side_effects=True, vmem_limit_bytes=56 * 1024 * 1024
        ),
    )(tiles, row_live, col_live, row_order, source_init, receiver_init)


def solution(mesh):
    placed = (
        P(None, ("row", "col"), None),
        P(None, ("row", "col")),
        P(None, ("row", "col")),
        P(),
        P(("row", "col"), None),
        P(("row", "col"), None),
    )
    return jax.shard_map(
        functools.partial(local, mesh.shape["row"], mesh.shape["col"]),
        mesh=mesh,
        in_specs=placed,
        out_specs=(P(("row", "col"), None), P(("row", "col"), None)),
        check_vma=False,
    )
```

time: 150 us -> 102 us (0.68)
  Pallas kernels: 0 us -> 96.5 us
  waiting for transfers between devices: 94.8 us -> 0 us
  matrix products: 29.1 us -> 0 us
  starting transfers between devices: 9.32 us -> 0 us
  other arithmetic: 5.44 us -> 0 us
  local copies, waits for them, and re-layouts: 9.34 us -> 4.52 us
    pallas_call x0 -> x1, Pallas kernels: none -> 96.5 us  [local(): pl.pallas_call(functools.partial(kernel, nr, nc), out_shape=(jax.ShapeDty...]
    ppermute x3 -> x0, waiting for transfers between devices: 55.4 us -> none  [from_behind(): return lax.ppermute(block, axis, route)]
    all_to_all x2 -> x0, waiting for transfers between devices: 39.4 us -> none  [the longest x1 20.2 us: reassign(): lax.all_to_all(rec_block.reshape(1, block_rows, rank_width), 'row', split...]
    dot_general x24 -> x0, matrix products: 29.1 us -> none  [the longest x8 11.8 us: fit_dense(): lax.dot_general(src_half, rec_half, (((1,), (1,)), ((), ())), preferred_e...]
    all_to_all x2 -> x0, starting transfers between devices: 8.65 us -> none  [the longest x1 4.42 us: reassign(): lax.all_to_all(pieces, 'row', split_axis=0, concat_axis=1, tiled=True)]
    convert_element_type x3 -> x0, other arithmetic: 3.05 us -> none  [the longest x1 1.28 us: fit_dense(): rec_half = rec_block.astype(jnp.bfloat16)]
    gather x1 -> x0, local copies, waits for them, and re-layouts: 2.81 us -> none  [reassign(): pieces = jnp.take(pieces, row_order, axis=0)]
    select_n x2 -> x0, other arithmetic: 2.38 us -> none  [reassign(): pieces = jnp.take(pieces, row_order, axis=0)]
  transfers between devices with their start and end apart: 5 -> 0, of which waited for: 5 -> 0; matrix products, arithmetic and copies ran while one was open for 3% -> 0% of each run, Pallas kernels for 0% -> 0%
where the time goes in v1:
time: 102 us
  Pallas kernels  96.5 us (95%)
  local copies, waits for them, and re-layouts  4.52 us (4%)
    pallas_call x1, Pallas kernels, local(): pl.pallas_call(functools.partial(kernel, nr, nc), out_shape=(jax.ShapeDty...  96.5 us
    unnamed x2, local copies, waits for them, and re-layouts  4.52 us

profile of v1, /device:TPU:0, one launch (start us, length us, event | category | flops | bytes accessed | tf_op | source)
XLA Modules:
  0.0 101.7 jit_solution(15714195741315128148)
XLA Ops:
  0.6 96.5 %shard_map.77 = (f32[1024,256]{1,0:T(8,128)}, f32[1024,256]{1,0:T(8,128)}) custom-call(bf16[4,1024,1024]{2,1,0:T(8,128)(2,1)} %tiles.1, s32[4,1024]{1,0:T(4,128)} %row_live.1, s32[4,1024]{1,0:T(4,128)} %col_live.1, s32[8]{0:T(128)} %order.1, f32[1024,256]{1,0:T(8,128)} %src_in.1, f32[1024,256]{1,0:T(8,128)} %rec_in.1), custom_call_target="tpu_custom_call" | custom-call | tf_op jit(solution)/shard_map/pallas_call | solution.py:177
  97.2 2.3 %copy.10 = f32[1024,256]{1,0:T(8,128)} copy(f32[1024,256]{1,0:T(8,128)} %get-tuple-element.4) | data formatting | bytes 2097152
  99.4 2.3 %copy.11 = f32[1024,256]{1,0:T(8,128)} copy(f32[1024,256]{1,0:T(8,128)} %get-tuple-element.5) | data formatting | bytes 2097152
